TPU v7x, 128 devices: a whole 4x4x4 slice. The times are simulated.
128 devices in a mesh: slab: 16 (over z, y), blk: 8 (over x, core).
Axes of the slice: x: 4, y: 4, z: 4, core: 2. Of those that a mesh axis runs over, the one named last changes fastest.
Arguments:
- positions: float32 [4096, 3, 128], P(('slab', 'blk')), may hold values from 0 to 1
- radius: float32 [4096, 128], P(('slab', 'blk')), may hold values from 0.15 to 0.3
- velocity: float32 [4096, 3, 128], P(('slab', 'blk')), may hold values from -3 to 3
- old_force: float32 [4096, 3, 128], P(('slab', 'blk')), may hold values from -6 to 6
- neighbours: int32 [4096, 16], P(('slab', 'blk')), may hold values from 0 to 47, as said below
- tile_count: int32 [4096], P(('slab', 'blk')), may hold values from 0 to 16
Outputs:
- new_positions: float32 [4096, 3, 128], P(('slab', 'blk'))
- new_velocity: float32 [4096, 3, 128], P(('slab', 'blk'))
- new_force: float32 [4096, 3, 128], P(('slab', 'blk'))
Inputs may be any that keep to these rules, and one draw needn't show every extreme that they name: neighbours[i, k] indexes the candidate list of bin i's group; it never names bin i itself, and names no candidate of a missing slab at the drum's ends.
All inputs are finite; a program needn't handle non-finite values.
Results may differ from a plain program's by a relative error of at most 0.0003.
Values sent between devices are 32-bit elements; how exact they have to be, the bound alone decides.
No kernel may reach another device: no remote copies, remote signals or barrier semaphores. Data moves between devices by JAX's collectives and lax.ppermute only.
A program may use at most 64 MiB of HBM per device.

v0:
```python
import functools

import jax
import jax.numpy as jnp
from jax import lax
from jax.experimental import pallas as pl
from jax.experimental.pallas import tpu as pltpu
from jax.sharding import PartitionSpec as P

GHOSTS = 8
TIMESTEP = 0.2
TINY = 1e-25
TILES = 4
BINS = 32
DEPTH = 48
END = BINS * 128
PLACES = 8192
HALVES = 8
F32 = jnp.float32
BF16 = jnp.bfloat16


def rounded(value):
    return value.astype(BF16).astype(F32)


def split3(value):
    high = rounded(value)
    middle = rounded(value - high)
    return high, middle, value - high - middle


def iotas(rows):
    shape = (rows, 128)
    return lax.broadcasted_iota(jnp.int32, shape, 0), lax.broadcasted_iota(jnp.int32, shape, 1)


def widened(value):
    rows, lanes = value.shape
    return jnp.concatenate([value, jnp.zeros((rows, 128 - lanes), value.dtype)], axis=1)


def table_of(weight, span):
    row, lane = iotas(BINS)
    step = jnp.where(weight > 0.0, row * 128 + lane, END)
    for s in (1, 2, 4, 8, 16, 32)[:span]:
        ahead = pltpu.roll(step, 128 - s, 1)
        step = jnp.minimum(step, jnp.where(lane + s < 128, ahead, END))
    later = jnp.broadcast_to(step[:, :1], (BINS, 128))
    later = jnp.where(row + 1 < BINS, pltpu.roll(later, BINS - 1, 0), END)
    for s in (1, 2, 4, 8, 16):
        ahead = pltpu.roll(later, BINS - s, 0)
        later = jnp.minimum(later, jnp.where(row + s < BINS, ahead, END))
    live = jnp.sum(jnp.where(weight > 0.0, 1.0, 0.0), axis=1, keepdims=True)
    live = jnp.broadcast_to(jnp.sum(live, axis=0, keepdims=True), (8, 128)).astype(jnp.int32)
    tail, _ = iotas(8)
    tail = jnp.where(tail == 1, live, END)
    return jnp.concatenate([jnp.minimum(step, later) + PLACES * weight.astype(jnp.int32), tail])


def prologue_kernel(slots, planes, packed, table):
    for c in range(4):
        packed[:BINS, c, :] = planes[c]
    slot = lax.broadcasted_iota(jnp.int32, (slots, 128), 0).astype(F32)
    marked = jnp.where(slot < planes[4, pl.ds(BINS - 1, 1), :], planes[4, :slots, :], -1.0)
    marked = jnp.transpose(marked)[:BINS]
    row, lane = iotas(BINS)
    candidate = lane.astype(F32)
    counts = jnp.zeros((BINS, 128), F32)
    for k in range(slots):
        counts = counts + jnp.where(marked[:, k : k + 1] == candidate, 1.0, 0.0)
    for n in range(BINS // 4):
        packed[BINS + n] = counts[4 * n : 4 * n + 4]
    inner = jnp.where(lane < BINS, pltpu.roll(counts, 128 - GHOSTS, 1), 0.0)
    mirror = widened(jnp.transpose(inner)[:BINS])
    pairs = jnp.where(lane > row, inner + mirror, 0.0)
    table[...] = table_of(jnp.where(lane == row, 1.0, pairs), 5)


def write_rows(packed, base, left, right, moment):
    span = pl.ds(base, BINS)
    radius = packed[:BINS, 3, :]
    sigma = jnp.sqrt(10.0 * radius)
    one = jnp.ones((BINS, 128), F32)
    zero = jnp.zeros((BINS, 128), F32)
    norm = zero
    for c in range(3):
        place = packed[:BINS, c, :] - 0.5
        norm = norm + place * place
        right[span, c, :] = -2.0 * place
        moment[span, c, :] = sigma * place
        if left is not None:
            left[span, c, :] = place
    moment[span, 3, :] = sigma
    right[span, 3, :] = one
    right[span, 4, :] = norm + 0.0025
    for t in (5, 6, 7):
        right[span, t, :] = zero
    for t in (4, 5, 6, 7):
        moment[span, t, :] = zero
    if left is not None:
        left[span, 3, :] = norm
        left[span, 4, :] = one
        left[span, 5, :] = radius
        left[span, 6, :] = zero
        left[span, 7, :] = zero


def right_operands(n, right, moment, right_b, moment_b):
    high, middle, low = split3(right[n])
    right_b[n] = jnp.concatenate([high, middle, high, middle, low, high]).astype(BF16)
    high, middle, low = split3(moment[n])
    moment_b[n] = jnp.concatenate([high + pltpu.roll(middle, 4, 0), low]).astype(BF16)


def left_operand(n, left):
    high, middle, low = split3(left[n])
    return jnp.transpose(jnp.concatenate([high, high, middle, middle, high, low])).astype(BF16)


def run_tiles(table, target, lt, ra, right, moment, packed_row, acc_a, acc_b, scratch):
    s0, s1, p0, p1 = scratch
    s0[...] = jnp.ones_like(s0)
    p0[...] = jnp.zeros_like(p0)

    def bins(f):
        return jnp.minimum(f >> 7, BINS - 1), f & 127

    def times(f):
        return (table[f >> 7, f & 127] >> 13).astype(F32)

    def distances(tiles, s_ref):
        for n, f in enumerate(tiles):
            a, b = bins(f)
            s_ref[n] = jnp.dot(lt[a], right[b], preferred_element_type=F32)

    def weights(tiles, s_ref, p_ref):
        for n, f in enumerate(tiles):
            a, b = bins(f)
            r_b = packed_row(b)
            for g in range(8):
                rows = slice(16 * g, 16 * g + 16)
                s = s_ref[n, rows, :]
                v = jnp.maximum((ra[a, rows, :] + r_b) * lax.rsqrt(s) - 1.0, TINY)
                square = v * v
                w = square * lax.rsqrt(square + v)
                high = w.astype(BF16)
                low = (w - high.astype(F32)).astype(BF16)
                p_ref[n, 0, rows, :] = high
                p_ref[n, 1, rows, :] = low

    def forces(tiles, p_ref):
        for q in range(0, TILES, 2):
            a1, b1 = bins(tiles[q])
            a2, b2 = bins(tiles[q + 1])
            high1, low1 = p_ref[q, 0], p_ref[q, 1]
            high2, low2 = p_ref[q + 1, 0], p_ref[q + 1, 1]
            scale1, scale2 = times(tiles[q]), times(tiles[q + 1])
            if acc_b is not None:
                c1, c2 = target(a1, b1), target(a2, b2)
                m = jnp.concatenate([moment[a1], moment[a2]], axis=0)
                both = jnp.concatenate(
                    [
                        jnp.concatenate([high1, high2], axis=1),
                        jnp.concatenate([low1, low2], axis=1),
                    ],
                    axis=0,
                )
                out = jnp.dot(
                    jnp.concatenate([m, m], axis=1), both, preferred_element_type=F32
                )
                acc_b[c1] += scale1 * out[:16, :128]
                acc_b[c2] += scale2 * out[16:, 128:]
            m = jnp.concatenate([moment[b1], moment[b2]], axis=0)
            out = lax.dot_general(
                jnp.concatenate([m, m], axis=1),
                jnp.concatenate(
                    [
                        jnp.concatenate([high1, low1], axis=1),
                        jnp.concatenate([high2, low2], axis=1),
                    ],
                    axis=0,
                ),
                (((1,), (1,)), ((), ())),
                preferred_element_type=F32,
            )
            acc_a[a1] += scale1 * out[:16, :128]
            acc_a[a2] += scale2 * out[16:, 128:]

    def following(f):
        return table[f >> 7, f & 127] & (PLACES - 1)

    def draw(f):
        tiles = []
        for _ in range(TILES):
            tiles.append(f)
            f = following(jnp.minimum(f + 1, END))
        return f, tuple(tiles)

    none = (jnp.int32(END),) * TILES

    def body(count, _, carry):
        f, second, third = carry
        for half in range(count):
            f, first = draw(f)
            s_from, s_to, p_from, p_to = (s0, s1, p0, p1) if half % 2 == 0 else (s1, s0, p1, p0)
            forces(third, p_from)
            weights(second, s_from, p_to)
            distances(first, s_to)
            second, third = first, second
        return f, second, third

    live = table[BINS + 1, 0]
    halves = (live + TILES - 1) // TILES + 2
    long = halves // HALVES
    short = (halves - long * HALVES + 1) // 2
    carry = (following(jnp.int32(0)), none, none)
    carry = lax.fori_loop(0, long, functools.partial(body, HALVES), carry)
    lax.fori_loop(0, short, functools.partial(body, 2), carry)


def own_kernel(table_v, packed, acc, lt, ra, new_positions, places, sent, table, loaded, left, right, moment, right_b, moment_b, acc_b, *scratch):
    load = pltpu.make_async_copy(table_v, table, loaded)
    load.start()
    for c in range(3):
        places[c] = packed[:BINS, c, :]
    send = pltpu.make_async_copy(places, new_positions, sent)
    send.start()
    write_rows(packed, 0, left, right, moment)
    depth = lax.broadcasted_iota(jnp.int32, (DEPTH, 128), 0)
    choose = ((depth == 5) | (depth == 21) | (depth == 45)).astype(BF16)

    def turn(n, carry):
        right_operands(n, right, moment, right_b, moment_b)
        columns = left_operand(n, left)
        lt[n] = columns
        ra[n] = jnp.dot(columns, choose, preferred_element_type=F32)
        return carry

    lax.fori_loop(0, BINS, turn, 0, unroll=8)
    acc[...] = jnp.zeros_like(acc)
    acc_b[...] = jnp.zeros_like(acc_b)
    load.wait()
    run_tiles(table, lambda a, b: jnp.where(a == b, BINS, b), lt, ra, right_b, moment_b,
              lambda b: packed[b, pl.ds(3, 1), :], acc, acc_b, scratch)
    acc[...] += acc_b[:BINS]
    send.wait()


def cross_kernel(upward, even, odd, packed, velocity, old_force, acc_in, lt, ra,
                 new_velocity, new_force, right, moment, right_b, moment_b, radii, acc,
                 table_v, table, loaded, *scratch):
    is_up = upward[0] > 0
    row, lane = iotas(BINS)

    def counts_of(ref):
        return jnp.concatenate([ref[BINS + n] for n in range(BINS // 4)])

    mine = counts_of(packed)
    lower = jnp.where((lane >= BINS - GHOSTS) & (lane < BINS), pltpu.roll(mine, BINS - GHOSTS, 1), 0.0)
    upper = jnp.where(lane < GHOSTS, pltpu.roll(mine, 128 - BINS - GHOSTS, 1), 0.0)
    blank = jnp.zeros((BINS - GHOSTS, 128), F32)

    def with_partner(counts, above):
        flipped = widened(jnp.transpose(counts))
        above_part = upper + jnp.concatenate([blank, flipped[:GHOSTS]])
        below_part = lower + jnp.concatenate([flipped[BINS + GHOSTS : BINS + 2 * GHOSTS], blank])
        return jnp.where(above, above_part, below_part)

    by_even = with_partner(counts_of(even), is_up)
    by_odd = with_partner(counts_of(odd), jnp.logical_not(is_up))
    table_v[...] = table_of(by_even + pltpu.roll(by_odd, BINS, 1), 6)
    load = pltpu.make_async_copy(table_v, table, loaded)
    load.start()
    write_rows(even, 0, None, right, moment)
    write_rows(odd, BINS, None, right, moment)
    radii[:BINS] = even[:BINS, pl.ds(3, 1), :]
    radii[BINS:] = odd[:BINS, pl.ds(3, 1), :]

    def turn(n, carry):
        right_operands(n, right, moment, right_b, moment_b)
        return carry

    lax.fori_loop(0, 2 * BINS, turn, 0, unroll=8)
    acc[...] = acc_in[...]
    load.wait()
    run_tiles(table, None, lt, ra, right_b, moment_b, lambda b: radii[b], acc, None, scratch)
    radius = packed[:BINS, 3, :]
    sigma = jnp.sqrt(10.0 * radius)
    scale = 1.0 / (125.0 * radius * radius * radius)

    def gathered(c):
        return acc[:, c, :] + acc[:, 4 + c, :] + acc[:, 8 + c, :]

    total = gathered(3)
    for c in range(3):
        force = sigma * ((packed[:BINS, c, :] - 0.5) * total - gathered(c))
        new_force[c] = force
        gravity = -0.5 if c == 1 else 0.0
        accel = (old_force[c] * scale + gravity) + (force * scale + gravity)
        new_velocity[c] = velocity[c] + 0.5 * TIMESTEP * accel


VMEM = pl.BlockSpec(memory_space=pltpu.VMEM)
SMEM = pl.BlockSpec(memory_space=pltpu.SMEM)
HBM = pl.BlockSpec(memory_space=pltpu.HBM)


def pipeline_scratch():
    return [
        pltpu.VMEM((TILES, 128, 128), F32),
        pltpu.VMEM((TILES, 128, 128), F32),
        pltpu.VMEM((TILES, 2, 128, 128), BF16),
        pltpu.VMEM((TILES, 2, 128, 128), BF16),
    ]


def local(positions, radius, velocity, old_force, neighbours, tile_count):
    def by_component(cells):
        return jnp.transpose(cells, (1, 0, 2))

    positions, velocity, old_force = map(by_component, (positions, velocity, old_force))
    cells = jax.ShapeDtypeStruct((3, BINS, 128), F32)
    slots = neighbours.shape[1]
    component = lax.broadcasted_iota(jnp.int32, (5, BINS, 128), 0)
    five = ((0, 2), (0, 0), (0, 0))
    each_radius = jnp.where(component < 3, radius[None], 1.0)
    accel = jnp.pad(old_force, five) / (125.0 * each_radius * each_radius * each_radius)
    accel = accel + jnp.where(component == 1, -0.5, 0.0)
    moved = jnp.pad(positions, five) + TIMESTEP * jnp.pad(velocity, five) + 0.5 * TIMESTEP * TIMESTEP * accel
    planes = jnp.where(component < 3, moved, radius[None])
    listed = jnp.pad(neighbours.T[None], ((4, 0), (0, BINS - slots), (0, 128 - BINS)))
    counted = jnp.pad(tile_count[None, None], ((4, 0), (BINS - 1, 0), (0, 128 - BINS)))
    planes = jnp.where(component < 4, planes, (listed + counted).astype(F32))
    packed, own_table = pl.pallas_call(
        functools.partial(prologue_kernel, slots),
        out_shape=(
            jax.ShapeDtypeStruct((BINS + 8, 4, 128), F32),
            jax.ShapeDtypeStruct((BINS + 8, 128), jnp.int32),
        ),
        in_specs=[VMEM],
        out_specs=(VMEM,) * 2,
        compiler_params=pltpu.CompilerParams(vmem_limit_bytes=8 << 20),
        name="prologue",
    )(planes)

    slabs = lax.axis_size("slab")
    swap_even = [(i + d, i + 1 - d) for i in range(0, slabs - 1, 2) for d in (0, 1)]
    swap_odd = [(i + d, i + 1 - d) for i in range(1, slabs - 1, 2) for d in (0, 1)]
    even = lax.ppermute(packed, "slab", swap_even)
    odd = lax.ppermute(packed, "slab", swap_odd)

    acc, lt, ra, new_positions = pl.pallas_call(
        own_kernel,
        out_shape=(
            jax.ShapeDtypeStruct((BINS, 16, 128), F32),
            jax.ShapeDtypeStruct((BINS, 128, DEPTH), BF16),
            jax.ShapeDtypeStruct((BINS, 128, 128), F32),
            cells,
        ),
        in_specs=[VMEM, VMEM],
        out_specs=(VMEM, VMEM, VMEM, HBM),
        scratch_shapes=[
            pltpu.VMEM((3, BINS, 128), F32),
            pltpu.SemaphoreType.DMA,
            pltpu.SMEM((BINS + 8, 128), jnp.int32),
            pltpu.SemaphoreType.DMA,
            pltpu.VMEM((BINS, 8, 128), F32),
            pltpu.VMEM((BINS, 8, 128), F32),
            pltpu.VMEM((BINS, 8, 128), F32),
            pltpu.VMEM((BINS, DEPTH, 128), BF16),
            pltpu.VMEM((BINS, 16, 128), BF16),
            pltpu.VMEM((BINS + 1, 16, 128), F32),
            *pipeline_scratch(),
        ],
        compiler_params=pltpu.CompilerParams(vmem_limit_bytes=16 << 20),
        cost_estimate=pl.CostEstimate(flops=10**9, bytes_accessed=10**6, transcendentals=0),
        name="own_tiles",
    )(own_table, packed)

    upward = (1 - lax.axis_index("slab") % 2).astype(jnp.int32)[None]
    new_velocity, new_force = pl.pallas_call(
        cross_kernel,
        out_shape=(cells, cells),
        in_specs=[SMEM] + [VMEM] * 8,
        out_specs=(VMEM, VMEM),
        scratch_shapes=[
            pltpu.VMEM((2 * BINS, 8, 128), F32),
            pltpu.VMEM((2 * BINS, 8, 128), F32),
            pltpu.VMEM((2 * BINS, DEPTH, 128), BF16),
            pltpu.VMEM((2 * BINS, 16, 128), BF16),
            pltpu.VMEM((2 * BINS, 1, 128), F32),
            pltpu.VMEM((BINS, 16, 128), F32),
            pltpu.VMEM((BINS + 8, 128), jnp.int32),
            pltpu.SMEM((BINS + 8, 128), jnp.int32),
            pltpu.SemaphoreType.DMA,
            *pipeline_scratch(),
        ],
        compiler_params=pltpu.CompilerParams(vmem_limit_bytes=16 << 20),
        cost_estimate=pl.CostEstimate(flops=10**9, bytes_accessed=10**6, transcendentals=0),
        name="cross_tiles",
    )(upward, even, odd, packed, velocity, old_force, acc, lt, ra)
    return tuple(map(by_component, (new_positions, new_velocity, new_force)))


def solution(mesh):
    flat = P(("slab", "blk"))
    rows = P(("slab", "blk"), None)
    cells = P(("slab", "blk"), None, None)
    return jax.shard_map(
        local,
        mesh=mesh,
        in_specs=(cells, rows, cells, cells, rows, flat),
        out_specs=(cells, cells, cells),
        check_vma=False,
    )
```

profile of v0, /device:TPU:102, one launch (start us, length us, event | category | flops | bytes accessed | tf_op | source)
XLA Modules:
  0.0 27.5 jit_solution(11715674750938671139)
XLA Ops:
  0.6 0.0 copy-start
  0.6 0.0 copy-start.1
  0.7 1.0 %convert_select_fusion.planes = f32[5,32,128]{2,1,0:T(8,128)S(1)} fusion(s32[1,1,32]{2,1,0:T(1,128)} %bitcast.17, s32[1,16,32]{2,1,0:T(8,128)} %bitcast.16, f32[3,32,128]{2,1,0:T(8,128)} %bitcast.11, f32[3,32,128]{2,1,0:T(8,128)} %bitcast.13, f32[3,32,128]{2,1,0:T(8,128)} %bitcast.15, f32[5]{0:T(128)S(1)} %compare_select_fusion, f32[32,128]{1,0:T(8,128)} %param.7, ...), kind=kLoop, calls=%fused_computation.7 | loop fusion | flops 286720 | bytes 247966 | tf_op jit(solution)/shard_map/jit(_where)/select_n | solution.py:334
  1.7 0.9 %prologue.1 = (f32[40,4,128]{2,1,0:T(4,128)S(1)}, s32[40,128]{1,0:T(8,128)S(1)}) custom-call(f32[5,32,128]{2,1,0:T(8,128)S(1)} %convert_select_fusion.planes), custom_call_target="tpu_custom_call" | custom-call | tf_op jit(solution)/shard_map/prologue/pallas_call | solution.py:335
  2.5 1.7 %collective-permute-start = (f32[40,4,128]{2,1,0:T(4,128)S(1)}, f32[40,4,128]{2,1,0:T(4,128)S(1)}, u32[]{:S(2)}, u32[]{:S(2)}) collective-permute-start(f32[40,4,128]{2,1,0:T(4,128)S(1)} %get-tuple-element.12.packed), channel_id=1, source_target_pairs={{0,8},{8,0},{16,24},{24,16},{32,40},{40,32},{48,56},{56,48},{64,72... | collective-permute-start | bytes 245768 | tf_op jit(solution)/shard_map/ppermute | solution.py:350
  4.2 3.9 %collective-permute-start.1 = (f32[40,4,128]{2,1,0:T(4,128)S(1)}, f32[40,4,128]{2,1,0:T(4,128)S(1)}, u32[]{:S(2)}, u32[]{:S(2)}) collective-permute-start(f32[40,4,128]{2,1,0:T(4,128)S(1)} %get-tuple-element.12.packed), channel_id=1, source_target_pairs={{8,16},{16,8},{24,32},{32,24},{40,48},{48,40},{56,64},{64,56},{72,... | collective-permute-start | bytes 245768 | tf_op jit(solution)/shard_map/ppermute | solution.py:351
  8.1 10.2 %own_tiles.1 = (f32[32,16,128]{2,1,0:T(8,128)S(1)}, bf16[32,128,48]{2,1,0:T(8,128)(2,1)S(1)}, f32[32,128,128]{2,1,0:T(8,128)S(1)}, f32[3,32,128]{2,1,0:T(8,128)}) custom-call(s32[40,128]{1,0:T(8,128)S(1)} %get-tuple-element.11.table_v, f32[40,4,128]{2,1,0:T(4,128)S(1)} %get-tuple-element.12.packed), custom_call_target="tpu_custom_call" | custom-call | flops 1000000000 | bytes 1000000 | tf_op jit(solution)/shard_map/own_tiles/pallas_call | solution.py:353
  18.3 0.0 collective-permute-done.even
  18.3 0.0 collective-permute-done.1.odd
  18.3 0.0 copy-done
  18.4 0.0 copy-done.1
  18.4 9.1 %cross_tiles.1 = (f32[3,32,128]{2,1,0:T(8,128)}, f32[3,32,128]{2,1,0:T(8,128)}) custom-call(s32[1]{0:T(128)} %bitcast.7.upward, f32[40,4,128]{2,1,0:T(4,128)S(1)} %collective-permute-done.even, f32[40,4,128]{2,1,0:T(4,128)S(1)} %collective-permute-done.1.odd, f32[40,4,128]{2,1,0:T(4,128)S(1)} %get-tuple-element.12.packed, f32[3,32,128]{2,1,0:T(8,128)S(1)} %bitcast.14, ...), custom_call_target="tpu_custom_call" | custom-call | flops 1000000000 | bytes 1000000 | tf_op jit(solution)/shard_map/cross_tiles/pallas_call | solution.py:382
  (2 shorter events, 0.0 us)
Async XLA Ops:
  0.6 17.7 %copy-start = (f32[32,3,128]{2,0,1:T(8,128)S(1)}, f32[32,3,128]{2,0,1:T(8,128)}, u32[]{:S(2)}) copy-start(f32[32,3,128]{2,0,1:T(8,128)} %param.9) | copy-start | bytes 147460
  0.6 17.7 %copy-start.1 = (f32[32,3,128]{2,0,1:T(8,128)S(1)}, f32[32,3,128]{2,0,1:T(8,128)}, u32[]{:S(2)}) copy-start(f32[32,3,128]{2,0,1:T(8,128)} %param.8) | copy-start | bytes 147460
  2.5 15.8 %collective-permute-start = (f32[40,4,128]{2,1,0:T(4,128)S(1)}, f32[40,4,128]{2,1,0:T(4,128)S(1)}, u32[]{:S(2)}, u32[]{:S(2)}) collective-permute-start(f32[40,4,128]{2,1,0:T(4,128)S(1)} %get-tuple-element.12.packed), channel_id=1, source_target_pairs={{0,8},{8,0},{16,24},{24,16},{32,40},{40,32},{48,56},{56,48},{64,72... | collective-permute-start | bytes 245768 | tf_op jit(solution)/shard_map/ppermute | solution.py:350
  4.2 14.1 %collective-permute-start.1 = (f32[40,4,128]{2,1,0:T(4,128)S(1)}, f32[40,4,128]{2,1,0:T(4,128)S(1)}, u32[]{:S(2)}, u32[]{:S(2)}) collective-permute-start(f32[40,4,128]{2,1,0:T(4,128)S(1)} %get-tuple-element.12.packed), channel_id=1, source_target_pairs={{8,16},{16,8},{24,32},{32,24},{40,48},{48,40},{56,64},{64,56},{72,... | collective-permute-start | bytes 245768 | tf_op jit(solution)/shard_map/ppermute | solution.py:351
where the time goes:
time: 27.3 us; the launch traced here: 27.5 us
  Pallas kernels  20.2 us (74%)
  starting transfers between devices  5.57 us (20%)
  other arithmetic  0.99 us (4%)
  between operations  0.73 us (3%)
    pallas_call x1, Pallas kernels, local(): pl.pallas_call(own_kernel, out_shape=(jax.ShapeDtypeStruct((BINS, 16, 128...  10.2 us
    pallas_call x1, Pallas kernels, local(): pl.pallas_call(cross_kernel, out_shape=(cells, cells), in_specs=[SMEM] +...  9.13 us
    ppermute x1, starting transfers between devices, local(): odd = lax.ppermute(packed, 'slab', swap_odd)  3.92 us
    ppermute x1, starting transfers between devices, local(): even = lax.ppermute(packed, 'slab', swap_even)  1.65 us
    select_n x1, other arithmetic, local(): planes = jnp.where(component < 4, planes, (listed + counted).astype(F32))  0.98 us
    pallas_call x1, Pallas kernels, local(): pl.pallas_call(functools.partial(prologue_kernel, slots), out_shape=(jax....  0.88 us
  transfers between devices with their start and end apart: 2, of which 0 were waited for; matrix products, arithmetic and copies ran while one was open for 0% of the time, Pallas kernels for 37%

commit v1 on v0

--- a/solution.py
+++ b/solution.py
@@ -77,45 +77,33 @@
     table[...] = table_of(jnp.where(lane == row, 1.0, pairs), 5)
 
 
-def write_rows(packed, base, left, right, moment):
-    span = pl.ds(base, BINS)
-    radius = packed[:BINS, 3, :]
+def bin_rows(cell):
+    cell = jnp.concatenate([cell, jnp.zeros((4, 128), F32)])
+    row = lax.broadcasted_iota(jnp.int32, (8, 128), 0)
+    radius = cell[3:4]
     sigma = jnp.sqrt(10.0 * radius)
-    one = jnp.ones((BINS, 128), F32)
-    zero = jnp.zeros((BINS, 128), F32)
-    norm = zero
-    for c in range(3):
-        place = packed[:BINS, c, :] - 0.5
-        norm = norm + place * place
-        right[span, c, :] = -2.0 * place
-        moment[span, c, :] = sigma * place
-        if left is not None:
-            left[span, c, :] = place
-    moment[span, 3, :] = sigma
-    right[span, 3, :] = one
-    right[span, 4, :] = norm + 0.0025
-    for t in (5, 6, 7):
-        right[span, t, :] = zero
-    for t in (4, 5, 6, 7):
-        moment[span, t, :] = zero
-    if left is not None:
-        left[span, 3, :] = norm
-        left[span, 4, :] = one
-        left[span, 5, :] = radius
-        left[span, 6, :] = zero
-        left[span, 7, :] = zero
-
-
-def right_operands(n, right, moment, right_b, moment_b):
-    high, middle, low = split3(right[n])
-    right_b[n] = jnp.concatenate([high, middle, high, middle, low, high]).astype(BF16)
-    high, middle, low = split3(moment[n])
-    moment_b[n] = jnp.concatenate([high + pltpu.roll(middle, 4, 0), low]).astype(BF16)
-
-
-def left_operand(n, left):
-    high, middle, low = split3(left[n])
+    place = jnp.where(row < 3, cell - 0.5, 0.0)
+    square = place * place
+    norm = square[0:1] + square[1:2] + square[2:3]
+    right = jnp.where(row == 3, 1.0, jnp.where(row == 4, norm + 0.0025, -2.0 * place))
+    left = jnp.where(row == 3, norm, jnp.where(row == 4, 1.0, jnp.where(row == 5, radius, place)))
+    moment = sigma * jnp.where(row == 3, 1.0, place)
+    return right, left, moment
+
+
+def right_operand(rows):
+    high, middle, low = split3(rows)
+    return jnp.concatenate([high, middle, high, middle, low, high]).astype(BF16)
+
+
+def left_operand(rows):
+    high, middle, low = split3(rows)
     return jnp.transpose(jnp.concatenate([high, high, middle, middle, high, low])).astype(BF16)
+
+
+def moment_operand(rows):
+    high, middle, low = split3(rows)
+    return jnp.concatenate([high + pltpu.roll(middle, 4, 0), low]).astype(BF16)
 
 
 def run_tiles(table, target, lt, ra, right, moment, packed_row, acc_a, acc_b, scratch):
@@ -219,20 +207,21 @@
     lax.fori_loop(0, short, functools.partial(body, 2), carry)
 
 
-def own_kernel(table_v, packed, acc, lt, ra, new_positions, places, sent, table, loaded, left, right, moment, right_b, moment_b, acc_b, *scratch):
+def own_kernel(table_v, packed, acc, lt, ra, new_positions, places, sent, table, loaded, right_b, moment_b, acc_b, *scratch):
     load = pltpu.make_async_copy(table_v, table, loaded)
     load.start()
     for c in range(3):
         places[c] = packed[:BINS, c, :]
     send = pltpu.make_async_copy(places, new_positions, sent)
     send.start()
-    write_rows(packed, 0, left, right, moment)
     depth = lax.broadcasted_iota(jnp.int32, (DEPTH, 128), 0)
     choose = ((depth == 5) | (depth == 21) | (depth == 45)).astype(BF16)
 
     def turn(n, carry):
-        right_operands(n, right, moment, right_b, moment_b)
-        columns = left_operand(n, left)
+        right, left, moment = bin_rows(packed[n])
+        right_b[n] = right_operand(right)
+        moment_b[n] = moment_operand(moment)
+        columns = left_operand(left)
         lt[n] = columns
         ra[n] = jnp.dot(columns, choose, preferred_element_type=F32)
         return carry
@@ -248,7 +237,7 @@
 
 
 def cross_kernel(upward, even, odd, packed, velocity, old_force, acc_in, lt, ra,
-                 new_velocity, new_force, right, moment, right_b, moment_b, radii, acc,
+                 new_velocity, new_force, right_b, moment_b, radii, acc,
                  table_v, table, loaded, *scratch):
     is_up = upward[0] > 0
     row, lane = iotas(BINS)
@@ -272,16 +261,17 @@
     table_v[...] = table_of(by_even + pltpu.roll(by_odd, BINS, 1), 6)
     load = pltpu.make_async_copy(table_v, table, loaded)
     load.start()
-    write_rows(even, 0, None, right, moment)
-    write_rows(odd, BINS, None, right, moment)
-    radii[:BINS] = even[:BINS, pl.ds(3, 1), :]
-    radii[BINS:] = odd[:BINS, pl.ds(3, 1), :]
 
     def turn(n, carry):
-        right_operands(n, right, moment, right_b, moment_b)
+        for ref, base in ((even, 0), (odd, BINS)):
+            cell = ref[n]
+            right, _, moment = bin_rows(cell)
+            right_b[base + n] = right_operand(right)
+            moment_b[base + n] = moment_operand(moment)
+            radii[base + n] = cell[3:4]
         return carry
 
-    lax.fori_loop(0, 2 * BINS, turn, 0, unroll=8)
+    lax.fori_loop(0, BINS, turn, 0, unroll=4)
     acc[...] = acc_in[...]
     load.wait()
     run_tiles(table, None, lt, ra, right_b, moment_b, lambda b: radii[b], acc, None, scratch)
@@ -365,9 +355,6 @@
             pltpu.SemaphoreType.DMA,
             pltpu.SMEM((BINS + 8, 128), jnp.int32),
             pltpu.SemaphoreType.DMA,
-            pltpu.VMEM((BINS, 8, 128), F32),
-            pltpu.VMEM((BINS, 8, 128), F32),
-            pltpu.VMEM((BINS, 8, 128), F32),
             pltpu.VMEM((BINS, DEPTH, 128), BF16),
             pltpu.VMEM((BINS, 16, 128), BF16),
             pltpu.VMEM((BINS + 1, 16, 128), F32),
@@ -385,8 +372,6 @@
         in_specs=[SMEM] + [VMEM] * 8,
         out_specs=(VMEM, VMEM),
         scratch_shapes=[
-            pltpu.VMEM((2 * BINS, 8, 128), F32),
-            pltpu.VMEM((2 * BINS, 8, 128), F32),
             pltpu.VMEM((2 * BINS, DEPTH, 128), BF16),
             pltpu.VMEM((2 * BINS, 16, 128), BF16),
             pltpu.VMEM((2 * BINS, 1, 128), F32),

time: 27.3 us -> 27.5 us (level)
  the two profiles are of different devices: /device:TPU:102 before, /device:TPU:97 now
where the time goes in v1:
time: 27.5 us; the launch traced here: 27.6 us
  Pallas kernels  20.8 us (76%)
  starting transfers between devices  5.01 us (18%)
  other arithmetic  0.99 us (4%)
  between operations  0.73 us (3%)
    pallas_call x1, Pallas kernels, local(): pl.pallas_call(cross_kernel, out_shape=(cells, cells), in_specs=[SMEM] +...  10.4 us
    pallas_call x1, Pallas kernels, local(): pl.pallas_call(own_kernel, out_shape=(jax.ShapeDtypeStruct((BINS, 16, 128...  9.56 us
    ppermute x1, starting transfers between devices, local(): odd = lax.ppermute(packed, 'slab', swap_odd)  3.64 us
    ppermute x1, starting transfers between devices, local(): even = lax.ppermute(packed, 'slab', swap_even)  1.37 us
    select_n x1, other arithmetic, local(): planes = jnp.where(component < 4, planes, (listed + counted).astype(F32))  0.98 us
    pallas_call x1, Pallas kernels, local(): pl.pallas_call(functools.partial(prologue_kernel, slots), out_shape=(jax....  0.88 us
  transfers between devices with their start and end apart: 2, of which 0 were waited for; matrix products, arithmetic and copies ran while one was open for 0% of the time, Pallas kernels for 35%

profile of v1, /device:TPU:97, one launch (start us, length us, event | category | flops | bytes accessed | tf_op | source)
XLA Modules:
  0.0 27.6 jit_solution(4731794827111579236)
XLA Ops:
  0.6 0.0 copy-start
  0.6 0.0 copy-start.1
  0.7 1.0 %convert_select_fusion.planes = f32[5,32,128]{2,1,0:T(8,128)S(1)} fusion(s32[1,1,32]{2,1,0:T(1,128)} %bitcast.17, s32[1,16,32]{2,1,0:T(8,128)} %bitcast.16, f32[3,32,128]{2,1,0:T(8,128)} %bitcast.11, f32[3,32,128]{2,1,0:T(8,128)} %bitcast.13, f32[3,32,128]{2,1,0:T(8,128)} %bitcast.15, f32[5]{0:T(128)S(1)} %compare_select_fusion, f32[32,128]{1,0:T(8,128)} %param.7, ...), kind=kLoop, calls=%fused_computation.7 | loop fusion | flops 286720 | bytes 247966 | tf_op jit(solution)/shard_map/jit(_where)/select_n | solution.py:324
  1.7 0.9 %prologue.1 = (f32[40,4,128]{2,1,0:T(4,128)S(1)}, s32[40,128]{1,0:T(8,128)S(1)}) custom-call(f32[5,32,128]{2,1,0:T(8,128)S(1)} %convert_select_fusion.planes), custom_call_target="tpu_custom_call" | custom-call | tf_op jit(solution)/shard_map/prologue/pallas_call | solution.py:325
  2.5 1.4 %collective-permute-start = (f32[40,4,128]{2,1,0:T(4,128)S(1)}, f32[40,4,128]{2,1,0:T(4,128)S(1)}, u32[]{:S(2)}, u32[]{:S(2)}) collective-permute-start(f32[40,4,128]{2,1,0:T(4,128)S(1)} %get-tuple-element.12.packed), channel_id=1, source_target_pairs={{0,8},{8,0},{16,24},{24,16},{32,40},{40,32},{48,56},{56,48},{64,72... | collective-permute-start | bytes 245768 | tf_op jit(solution)/shard_map/ppermute | solution.py:340
  3.9 3.6 %collective-permute-start.1 = (f32[40,4,128]{2,1,0:T(4,128)S(1)}, f32[40,4,128]{2,1,0:T(4,128)S(1)}, u32[]{:S(2)}, u32[]{:S(2)}) collective-permute-start(f32[40,4,128]{2,1,0:T(4,128)S(1)} %get-tuple-element.12.packed), channel_id=1, source_target_pairs={{8,16},{16,8},{24,32},{32,24},{40,48},{48,40},{56,64},{64,56},{72,... | collective-permute-start | bytes 245768 | tf_op jit(solution)/shard_map/ppermute | solution.py:341
  7.6 9.6 %own_tiles.1 = (f32[32,16,128]{2,1,0:T(8,128)S(1)}, bf16[32,128,48]{2,1,0:T(8,128)(2,1)S(1)}, f32[32,128,128]{2,1,0:T(8,128)S(1)}, f32[3,32,128]{2,1,0:T(8,128)}) custom-call(s32[40,128]{1,0:T(8,128)S(1)} %get-tuple-element.11.table_v, f32[40,4,128]{2,1,0:T(4,128)S(1)} %get-tuple-element.12.packed), custom_call_target="tpu_custom_call" | custom-call | flops 1000000000 | bytes 1000000 | tf_op jit(solution)/shard_map/own_tiles/pallas_call | solution.py:343
  17.1 0.0 collective-permute-done.even
  17.2 0.0 collective-permute-done.1.odd
  17.2 0.0 copy-done
  17.2 0.0 copy-done.1
  17.2 10.4 %cross_tiles.1 = (f32[3,32,128]{2,1,0:T(8,128)}, f32[3,32,128]{2,1,0:T(8,128)}) custom-call(s32[1]{0:T(128)} %bitcast.7.upward, f32[40,4,128]{2,1,0:T(4,128)S(1)} %collective-permute-done.even, f32[40,4,128]{2,1,0:T(4,128)S(1)} %collective-permute-done.1.odd, f32[40,4,128]{2,1,0:T(4,128)S(1)} %get-tuple-element.12.packed, f32[3,32,128]{2,1,0:T(8,128)S(1)} %bitcast.14, ...), custom_call_target="tpu_custom_call" | custom-call | flops 1000000000 | bytes 1000000 | tf_op jit(solution)/shard_map/cross_tiles/pallas_call | solution.py:369
  (2 shorter events, 0.0 us)
Async XLA Ops:
  0.6 16.5 %copy-start = (f32[32,3,128]{2,0,1:T(8,128)S(1)}, f32[32,3,128]{2,0,1:T(8,128)}, u32[]{:S(2)}) copy-start(f32[32,3,128]{2,0,1:T(8,128)} %param.9) | copy-start | bytes 147460
  0.6 16.5 %copy-start.1 = (f32[32,3,128]{2,0,1:T(8,128)S(1)}, f32[32,3,128]{2,0,1:T(8,128)}, u32[]{:S(2)}) copy-start(f32[32,3,128]{2,0,1:T(8,128)} %param.8) | copy-start | bytes 147460
  2.5 14.6 %collective-permute-start = (f32[40,4,128]{2,1,0:T(4,128)S(1)}, f32[40,4,128]{2,1,0:T(4,128)S(1)}, u32[]{:S(2)}, u32[]{:S(2)}) collective-permute-start(f32[40,4,128]{2,1,0:T(4,128)S(1)} %get-tuple-element.12.packed), channel_id=1, source_target_pairs={{0,8},{8,0},{16,24},{24,16},{32,40},{40,32},{48,56},{56,48},{64,72... | collective-permute-start | bytes 245768 | tf_op jit(solution)/shard_map/ppermute | solution.py:340
  3.9 13.2 %collective-permute-start.1 = (f32[40,4,128]{2,1,0:T(4,128)S(1)}, f32[40,4,128]{2,1,0:T(4,128)S(1)}, u32[]{:S(2)}, u32[]{:S(2)}) collective-permute-start(f32[40,4,128]{2,1,0:T(4,128)S(1)} %get-tuple-element.12.packed), channel_id=1, source_target_pairs={{8,16},{16,8},{24,32},{32,24},{40,48},{48,40},{56,64},{64,56},{72,... | collective-permute-start | bytes 245768 | tf_op jit(solution)/shard_map/ppermute | solution.py:341

commit v2 on v1

--- a/solution.py
+++ b/solution.py
@@ -226,7 +226,7 @@
         ra[n] = jnp.dot(columns, choose, preferred_element_type=F32)
         return carry
 
-    lax.fori_loop(0, BINS, turn, 0, unroll=8)
+    lax.fori_loop(0, BINS, turn, 0, unroll=32)
     acc[...] = jnp.zeros_like(acc)
     acc_b[...] = jnp.zeros_like(acc_b)
     load.wait()
@@ -236,7 +236,7 @@
     send.wait()
 
 
-def cross_kernel(upward, even, odd, packed, velocity, old_force, acc_in, lt, ra,
+def cross_kernel(upward, odd, even, packed, velocity, old_force, acc_in, lt, ra,
                  new_velocity, new_force, right_b, moment_b, radii, acc,
                  table_v, table, loaded, *scratch):
     is_up = upward[0] > 0
@@ -271,23 +271,22 @@
             radii[base + n] = cell[3:4]
         return carry
 
-    lax.fori_loop(0, BINS, turn, 0, unroll=4)
+    lax.fori_loop(0, BINS, turn, 0, unroll=16)
     acc[...] = acc_in[...]
     load.wait()
     run_tiles(table, None, lt, ra, right_b, moment_b, lambda b: radii[b], acc, None, scratch)
+    for n in range(BINS):
+        cell = packed[n]
+        sums = acc[n]
+        sums = sums[0:4] + sums[4:8] + sums[8:12]
+        force = jnp.sqrt(10.0 * cell[3:4]) * ((cell - 0.5) * sums[3:4] - sums)
+        for c in range(3):
+            new_force[c, pl.ds(n, 1), :] = force[c : c + 1]
     radius = packed[:BINS, 3, :]
-    sigma = jnp.sqrt(10.0 * radius)
     scale = 1.0 / (125.0 * radius * radius * radius)
-
-    def gathered(c):
-        return acc[:, c, :] + acc[:, 4 + c, :] + acc[:, 8 + c, :]
-
-    total = gathered(3)
     for c in range(3):
-        force = sigma * ((packed[:BINS, c, :] - 0.5) * total - gathered(c))
-        new_force[c] = force
         gravity = -0.5 if c == 1 else 0.0
-        accel = (old_force[c] * scale + gravity) + (force * scale + gravity)
+        accel = (old_force[c] * scale + gravity) + (new_force[c] * scale + gravity)
         new_velocity[c] = velocity[c] + 0.5 * TIMESTEP * accel
 
 
@@ -384,7 +383,7 @@
         compiler_params=pltpu.CompilerParams(vmem_limit_bytes=16 << 20),
         cost_estimate=pl.CostEstimate(flops=10**9, bytes_accessed=10**6, transcendentals=0),
         name="cross_tiles",
-    )(upward, even, odd, packed, velocity, old_force, acc, lt, ra)
+    )(upward, odd, even, packed, velocity, old_force, acc, lt, ra)
     return tuple(map(by_component, (new_positions, new_velocity, new_force)))
 
 

time: 27.5 us -> 26.5 us (0.964)
  the two profiles are of different devices: /device:TPU:97 before, /device:TPU:44 now
where the time goes in v2:
time: 26.5 us; the launch traced here: 26.9 us
  Pallas kernels  20.2 us (76%)
  starting transfers between devices  4.99 us (19%)
  other arithmetic  0.99 us (4%)
  between operations  0.71 us (3%)
    pallas_call x1, Pallas kernels, local(): pl.pallas_call(own_kernel, out_shape=(jax.ShapeDtypeStruct((BINS, 16, 128...  9.97 us
    pallas_call x1, Pallas kernels, local(): pl.pallas_call(cross_kernel, out_shape=(cells, cells), in_specs=[SMEM] +...  9.37 us
    ppermute x1, starting transfers between devices, local(): odd = lax.ppermute(packed, 'slab', swap_odd)  3.48 us
    ppermute x1, starting transfers between devices, local(): even = lax.ppermute(packed, 'slab', swap_even)  1.51 us
    select_n x1, other arithmetic, local(): planes = jnp.where(component < 4, planes, (listed + counted).astype(F32))  0.98 us
    pallas_call x1, Pallas kernels, local(): pl.pallas_call(functools.partial(prologue_kernel, slots), out_shape=(jax....  0.88 us
  transfers between devices with their start and end apart: 2, of which 0 were waited for; matrix products, arithmetic and copies ran while one was open for 0% of the time, Pallas kernels for 37%

profile of v2, /device:TPU:44, one launch (start us, length us, event | category | flops | bytes accessed | tf_op | source)
XLA Modules:
  0.0 26.9 jit_solution(16199678646832111332)
XLA Ops:
  0.6 0.0 copy-start
  0.6 0.0 copy-start.1
  0.7 1.0 %convert_select_fusion.planes = f32[5,32,128]{2,1,0:T(8,128)S(1)} fusion(s32[1,1,32]{2,1,0:T(1,128)} %bitcast.17, s32[1,16,32]{2,1,0:T(8,128)} %bitcast.16, f32[3,32,128]{2,1,0:T(8,128)} %bitcast.11, f32[3,32,128]{2,1,0:T(8,128)} %bitcast.13, f32[3,32,128]{2,1,0:T(8,128)} %bitcast.15, f32[5]{0:T(128)S(1)} %compare_select_fusion, f32[32,128]{1,0:T(8,128)} %param.7, ...), kind=kLoop, calls=%fused_computation.7 | loop fusion | flops 286720 | bytes 247966 | tf_op jit(solution)/shard_map/jit(_where)/select_n | solution.py:323
  1.7 0.9 %prologue.1 = (f32[40,4,128]{2,1,0:T(4,128)S(1)}, s32[40,128]{1,0:T(8,128)S(1)}) custom-call(f32[5,32,128]{2,1,0:T(8,128)S(1)} %convert_select_fusion.planes), custom_call_target="tpu_custom_call" | custom-call | tf_op jit(solution)/shard_map/prologue/pallas_call | solution.py:324
  2.5 3.5 %collective-permute-start = (f32[40,4,128]{2,1,0:T(4,128)S(1)}, f32[40,4,128]{2,1,0:T(4,128)S(1)}, u32[]{:S(2)}, u32[]{:S(2)}) collective-permute-start(f32[40,4,128]{2,1,0:T(4,128)S(1)} %get-tuple-element.12.packed), channel_id=1, source_target_pairs={{8,16},{16,8},{24,32},{32,24},{40,48},{48,40},{56,64},{64,56},{72,... | collective-permute-start | bytes 245768 | tf_op jit(solution)/shard_map/ppermute | solution.py:340
  6.0 1.5 %collective-permute-start.1 = (f32[40,4,128]{2,1,0:T(4,128)S(1)}, f32[40,4,128]{2,1,0:T(4,128)S(1)}, u32[]{:S(2)}, u32[]{:S(2)}) collective-permute-start(f32[40,4,128]{2,1,0:T(4,128)S(1)} %get-tuple-element.12.packed), channel_id=1, source_target_pairs={{0,8},{8,0},{16,24},{24,16},{32,40},{40,32},{48,56},{56,48},{64,72... | collective-permute-start | bytes 245768 | tf_op jit(solution)/shard_map/ppermute | solution.py:339
  7.5 10.0 %own_tiles.1 = (f32[32,16,128]{2,1,0:T(8,128)S(1)}, bf16[32,128,48]{2,1,0:T(8,128)(2,1)S(1)}, f32[32,128,128]{2,1,0:T(8,128)S(1)}, f32[3,32,128]{2,1,0:T(8,128)}) custom-call(s32[40,128]{1,0:T(8,128)S(1)} %get-tuple-element.11.table_v, f32[40,4,128]{2,1,0:T(4,128)S(1)} %get-tuple-element.12.packed), custom_call_target="tpu_custom_call" | custom-call | flops 1000000000 | bytes 1000000 | tf_op jit(solution)/shard_map/own_tiles/pallas_call | solution.py:342
  17.5 0.0 collective-permute-done.odd
  17.5 0.0 collective-permute-done.1.even
  17.5 0.0 copy-done
  17.6 0.0 copy-done.1
  17.6 9.4 %cross_tiles.1 = (f32[3,32,128]{2,1,0:T(8,128)}, f32[3,32,128]{2,1,0:T(8,128)}) custom-call(s32[1]{0:T(128)} %bitcast.7.upward, f32[40,4,128]{2,1,0:T(4,128)S(1)} %collective-permute-done.odd, f32[40,4,128]{2,1,0:T(4,128)S(1)} %collective-permute-done.1.even, f32[40,4,128]{2,1,0:T(4,128)S(1)} %get-tuple-element.12.packed, f32[3,32,128]{2,1,0:T(8,128)S(1)} %bitcast.14, ...), custom_call_target="tpu_custom_call" | custom-call | flops 1000000000 | bytes 1000000 | tf_op jit(solution)/shard_map/cross_tiles/pallas_call | solution.py:368
  (2 shorter events, 0.0 us)
Async XLA Ops:
  0.6 16.9 %copy-start = (f32[32,3,128]{2,0,1:T(8,128)S(1)}, f32[32,3,128]{2,0,1:T(8,128)}, u32[]{:S(2)}) copy-start(f32[32,3,128]{2,0,1:T(8,128)} %param.9) | copy-start | bytes 147460
  0.6 16.9 %copy-start.1 = (f32[32,3,128]{2,0,1:T(8,128)S(1)}, f32[32,3,128]{2,0,1:T(8,128)}, u32[]{:S(2)}) copy-start(f32[32,3,128]{2,0,1:T(8,128)} %param.8) | copy-start | bytes 147460
  2.5 15.0 %collective-permute-start = (f32[40,4,128]{2,1,0:T(4,128)S(1)}, f32[40,4,128]{2,1,0:T(4,128)S(1)}, u32[]{:S(2)}, u32[]{:S(2)}) collective-permute-start(f32[40,4,128]{2,1,0:T(4,128)S(1)} %get-tuple-element.12.packed), channel_id=1, source_target_pairs={{8,16},{16,8},{24,32},{32,24},{40,48},{48,40},{56,64},{64,56},{72,... | collective-permute-start | bytes 245768 | tf_op jit(solution)/shard_map/ppermute | solution.py:340
  6.0 11.5 %collective-permute-start.1 = (f32[40,4,128]{2,1,0:T(4,128)S(1)}, f32[40,4,128]{2,1,0:T(4,128)S(1)}, u32[]{:S(2)}, u32[]{:S(2)}) collective-permute-start(f32[40,4,128]{2,1,0:T(4,128)S(1)} %get-tuple-element.12.packed), channel_id=1, source_target_pairs={{0,8},{8,0},{16,24},{24,16},{32,40},{40,32},{48,56},{56,48},{64,72... | collective-permute-start | bytes 245768 | tf_op jit(solution)/shard_map/ppermute | solution.py:339
